TPU v7x, 128 devices: a whole 4x4x4 slice. The times are simulated.
128 devices in a mesh: row: 8 (over z, core), col: 16 (over x, y).
Axes of the slice: x: 4, y: 4, z: 4, core: 2. Of those that a mesh axis runs over, the one named last changes fastest.
Arguments:
- activations: bfloat16 [8192, 8192], P('row', 'col'), may hold values from -6 to 6
- errors: bfloat16 [8192, 8192], P('row', 'col'), may hold values from -6 to 6
- act_proj: bfloat16 [8192, 128], P('col'), may hold values from -0.0625 to 0.0625
- err_proj: bfloat16 [8192, 128], P('col'), may hold values from -0.0625 to 0.0625
- lengths: int32 [8, 64], P('row'), may hold values from 1 to 256, 1024 in all within a row
- ridge: float32 [16384, 16384], P('row', 'col'), may hold values from -4 to 36, as said below
- pivot_inverse: float32 [2, 512, 512], replicated, may hold values from -1 to 1
Outputs:
- eliminated: float32 [16384, 16384], P('row', 'col')
Inputs may be any that keep to these rules, and one draw needn't show every extreme that they name: The lengths of one row group sum to 1024. `ridge`: Symmetric.
All inputs are finite; a program needn't handle non-finite values.
Results may differ from a plain program's by a relative error of at most 0.0074.
Values may be sent and summed in bfloat16 or wider, within the bound.
A program may use at most 128 MiB of HBM per device.

v0:
```python
import jax
import jax.numpy as jnp
from jax import lax
from jax.sharding import PartitionSpec as P


def together(arrays, axis):
    ends = [0]
    for a in arrays:
        ends.append(ends[-1] + a.size)
    running = lax.psum(jnp.concatenate([a.ravel() for a in arrays]), axis)
    return tuple((running[b:e].reshape(a.shape) for a, b, e in zip(arrays, ends, ends[1:])))


def joined_along(tiles, dim):
    tiles = jnp.moveaxis(tiles, 0, dim)
    lengths = tiles.shape
    return tiles.reshape(*lengths[:dim], lengths[dim] * lengths[dim + 1], *lengths[dim + 2 :])


def from_everyone(array, axis):
    copies = jnp.broadcast_to(array, (lax.axis_size(axis), *array.shape))
    return lax.all_to_all(copies, axis, split_axis=0, concat_axis=0, tiled=True)


def gathered_copies(array, axis, dim):
    return joined_along(from_everyone(array, axis), dim)


def spread_2(array, axis, root):
    mine = lax.axis_index(axis) == root
    return lax.psum(jnp.where(mine, array, jnp.zeros_like(array)), axis)


def as_sent(array):

    def short(part):
        return part.astype(jnp.bfloat16) if part.dtype == jnp.float32 else part

    return jax.tree.map(short, array)


def from_root(array, axis, root):
    return lax.dynamic_index_in_dim(lax.all_gather(array, axis), root, 0, keepdims=False)


def per_device(activations, errors, act_proj, err_proj, lengths, ridge, pivot_inverse):
    part_act = jnp.dot(activations, act_proj, preferred_element_type=jnp.float32)
    part_err = jnp.dot(errors, err_proj, preferred_element_type=jnp.float32)
    summed_act, summed_err = together((part_act, part_err), "col")
    proj_act = summed_act.astype(jnp.bfloat16)
    col_count = lax.axis_size("col")
    row_count = lax.axis_size("row")
    col_ratio = col_count // row_count
    col_idx = lax.axis_index("col")
    row_idx = lax.axis_index("row")
    proj_width = act_proj.shape[1]
    err_share = proj_width // col_count
    err_part = lax.dynamic_slice_in_dim(summed_err, col_idx * err_share, err_share, 1).astype(
        jnp.bfloat16
    )
    lengths_row = lengths[0]
    captions_dev = lengths_row.shape[0]
    tokens_dev = activations.shape[0]
    caption_end = jnp.cumsum(lengths_row)
    caption_start = caption_end - lengths_row
    positions = jnp.arange(tokens_dev, dtype=jnp.int32)[:, None]
    member = ((positions >= caption_start[None, :]) & (positions < caption_end[None, :])).astype(
        jnp.bfloat16
    )
    weighted = (member[:, :, None] * err_part[:, None, :]).reshape(
        tokens_dev, captions_dev * err_share
    )
    local_grads = lax.dot_general(
        weighted, proj_act, (((0,), (0,)), ((), ())), preferred_element_type=jnp.float32
    )
    local_grads = local_grads.reshape(captions_dev, err_share * proj_width).astype(jnp.bfloat16)
    col_grads = gathered_copies(local_grads, "row", 0)
    row_parts = []
    for column_step in range(col_ratio):
        row_parts.append(spread_2(col_grads, "col", row_idx * col_ratio + column_step))
    row_grads = jnp.concatenate(row_parts, axis=1)
    captions_all = col_grads.shape[0]
    gram_tile = lax.dot_general(
        row_grads, col_grads, (((0,), (0,)), ((), ())), preferred_element_type=jnp.float32
    )
    matrix = ridge + gram_tile / captions_all
    tile_rows, tile_cols = ridge.shape
    row_start = row_idx * tile_rows
    col_start = col_idx * tile_cols
    row_ids = row_start + jnp.arange(tile_rows, dtype=jnp.int32)
    col_ids = col_start + jnp.arange(tile_cols, dtype=jnp.int32)
    panel_width = pivot_inverse.shape[1]

    def apply_inverse(columns, start_col, inverse):
        result = jnp.dot(columns, inverse.T, precision=lax.Precision.HIGHEST)
        return jnp.where(row_ids[:, None] >= start_col, result, 0.0)

    first_panel = apply_inverse(matrix[:, 0:panel_width], 0, pivot_inverse[0])
    pivot_block = from_root(
        first_panel[panel_width : 2 * panel_width].astype(jnp.bfloat16), "row", 0
    ).astype(jnp.float32)
    lower_first = jnp.where(row_ids[:, None] >= panel_width, first_panel, 0.0)
    second_block = matrix[:, panel_width : 2 * panel_width] - jnp.dot(
        lower_first, pivot_block.T, precision=lax.Precision.HIGHEST
    )
    second_panel = apply_inverse(second_block, panel_width, pivot_inverse[1])
    both_panels = jnp.concatenate([first_panel, second_panel], axis=1)
    row_panel = spread_2(as_sent(both_panels), "col", 0).astype(both_panels.dtype)
    col_piece = lax.dynamic_slice_in_dim(row_panel, col_idx % col_ratio * tile_cols, tile_cols, 0)
    col_panel = spread_2(as_sent(col_piece), "row", col_idx // col_ratio).astype(col_piece.dtype)
    row_panel, col_panel = (row_panel, col_panel)
    current = matrix
    stop_col = 2 * panel_width
    lower_part = jnp.where(row_ids[:, None] >= stop_col, row_panel, 0.0)
    upper_part = jnp.where(col_ids[:, None] >= stop_col, col_panel, 0.0)
    current = current - jnp.dot(lower_part, upper_part.T, precision=lax.Precision.HIGHEST)
    offset = jnp.clip(0 - col_start, 0, tile_cols - (stop_col - 0))
    placed = lax.dynamic_update_slice(jnp.zeros_like(current), row_panel, (jnp.int32(0), offset))
    in_panel = (col_ids >= 0) & (col_ids < stop_col)
    current = jnp.where(in_panel[None, :], placed, current)
    above_panel = ((row_ids >= 0) & (row_ids < stop_col))[:, None] & (col_ids >= stop_col)[None, :]
    return jnp.where(above_panel, 0.0, current)


def solution(mesh):
    in_specs = (
        P("row", "col"),
        P("row", "col"),
        P("col", None),
        P("col", None),
        P("row", None),
        P("row", "col"),
        P(),
    )
    out_specs = P("row", "col")
    return jax.shard_map(
        per_device, mesh=mesh, in_specs=in_specs, out_specs=out_specs, check_vma=False
    )
```

profile of v0, /device:TPU:0, one launch (start us, length us, event | category | flops | bytes accessed | tf_op | source)
XLA Modules:
  0.0 489.5 jit_solution(14978960739428227277)
XLA Ops:
  6.5 0.0 copy-start
  6.5 1.2 copy-done
  7.8 0.0 copy-start.5
  7.8 1.3 convolution_bitcast_fusion
  9.1 1.7 convolution_bitcast_fusion.1
  10.8 0.1 pad_maximum_fusion
  10.8 87.9 %all-reduce.11 = bf16[262144]{0:T(1024)(128)(2,1)S(1)} all-reduce(f32[262144]{0:T(1024)S(1)} %pad_maximum_fusion), channel_id=1, replica_groups=mesh['row'=8,'col'=16] {'col'}, use_global_device_ids=true, to_apply=%region_1.0 | all-reduce | flops 262144 | bytes 1572864 | tf_op jit(solution)/shard_map/psum | solution.py:11
  98.8 0.1 constant_dynamic-slice_fusion
  98.9 0.1 copy.24
  99.0 0.0 copy-done.5
  99.1 0.1 copy.18
  99.1 0.1 reduce-window.4
  99.2 0.1 reduce
  99.4 0.1 fusion.36
  99.5 0.4 convolution_convert_fusion
  99.9 0.1 convert_element_type.36
  100.0 1.1 broadcast_in_dim.82
  101.1 5.2 %all-to-all-start = ((bf16[8,64,1024]{2,1,0:T(8,128)(2,1)}), bf16[8,64,1024]{2,1,0:T(8,128)(2,1)S(1)}, u32[]{:S(2)}, u32[]{:S(2)}) async-start(bf16[8,64,1024]{2,1,0:T(8,128)(2,1)} %broadcast_in_dim.82), calls=%async_computation | async-start | bytes 2097152 | tf_op jit(solution)/shard_map/all_to_all | solution.py:23
  106.3 0.0 all-reduce.10.cloned.1.call-start
  106.4 15.9 %all-to-all-done = bf16[8,64,1024]{2,1,0:T(8,128)(2,1)S(1)} async-done(((bf16[8,64,1024]{2,1,0:T(8,128)(2,1)}), bf16[8,64,1024]{2,1,0:T(8,128)(2,1)S(1)}, u32[]{:S(2)}, u32[]{:S(2)}) %all-to-all-start) | async-done | bytes 1048608 | tf_op jit(solution)/shard_map/all_to_all | solution.py:23
  122.3 1.5 broadcast_select_fusion.1
  123.8 0.0 all-reduce.10.cloned.1.call-update
  123.8 0.0 all-gather.3.cloned.1.call-start
  123.9 86.4 %all-reduce.10.cloned.1.call-done = (bf16[512,1024]{1,0:T(8,128)(2,1)}, bf16[512,1024]{1,0:T(8,128)(2,1)}) async-done(((bf16[512,1024]{1,0:T(8,128)(2,1)}, bf16[512,1024]{1,0:T(8,128)(2,1)}), (bf16[512,1024]{1,0:T(8,128)(2,1)}, bf16[512,1024]{1,0:T(8,128)(2,1)})) %all-reduce.10.cloned.1.call-update) | async-done | bytes 2097168 | tf_op jit(solution)/shard_map/psum | solution.py:32
  210.3 0.0 copy-start.4
  210.3 6.7 %multiply_add_fusion = f32[2048,1024]{1,0:T(8,128)S(1)} fusion(f32[2048,1024]{1,0:T(8,128)} %param.12, bf16[512,1024]{1,0:T(8,128)(2,1)S(1)} %bitcast.35, bf16[512,1024]{1,0:T(8,128)(2,1)} %get-tuple-element.5, bf16[512,1024]{1,0:T(8,128)(2,1)} %get-tuple-element.6), kind=kOutput, calls=%fused_computation.5 | convolution fusion | flops 2155872256 | bytes 19922944 | tf_op jit(solution)/shard_map/dot_general | solution.py:84
  217.0 0.0 copy-done.4
  217.0 0.0 copy-start.2
  217.0 8.3 %select_convert_fusion.1 = (bf16[2048,512]{1,0:T(8,128)(2,1)S(1)}, f32[2048,512]{1,0:T(8,128)}) fusion(pred[2048]{0:T(1024)(128)(4,1)S(1)} %fusion.40, f32[2,512,512]{2,1,0:T(8,128)S(1)} %copy-done.4, f32[2048,1024]{1,0:T(8,128)S(1)} %multiply_add_fusion), kind=kOutput, calls=%fused_computation.20 | convolution fusion | flops 6443499520 | bytes 11536384 | tf_op jit(solution)/shard_map/dot_general | solution.py:96
  225.3 0.0 copy-done.2
  225.3 0.9 slice.55
  226.2 0.0 all-gather.3.cloned.1.call-update
  226.2 0.2 all-reduce.6.cloned.1.call-start
  226.5 31.7 %all-gather.3.cloned.1.call-done = bf16[4096,512]{1,0:T(8,128)(2,1)} async-done(((bf16[512,512]{1,0:T(8,128)(2,1)}), bf16[4096,512]{1,0:T(8,128)(2,1)}) %all-gather.3.cloned.1.call-update) | async-done | bytes 4194320 | tf_op jit(solution)/shard_map/all_gather | solution.py:44
  258.2 0.0 copy-start.3
  258.2 5.7 %fusion.9 = f32[2048,512]{1,0:T(8,128)S(1)} fusion(f32[2048,512]{1,0:T(8,128)} %get-tuple-element.10, pred[2048]{0:T(1024)(128)(4,1)S(1)} %fusion.38, pred[2048]{0:T(1024)(128)(4,1)S(1)} %fusion.40, bf16[4096,512]{1,0:T(8,128)(2,1)} %all-gather.3.cloned.1.call-done), kind=kOutput, calls=%fused_computation.15 | convolution fusion | flops 6444548096 | bytes 8916992 | tf_op jit(solution)/shard_map/dot_general | solution.py:104
  263.9 0.0 copy-done.3
  263.9 8.1 %select_convert_fusion = bf16[2048,512]{1,0:T(8,128)(2,1)S(1)} fusion(f32[2048,512]{1,0:T(8,128)S(1)} %fusion.9, f32[2048,1024]{1,0:T(8,128)S(1)} %copy-done.3, pred[2048]{0:T(1024)(128)(4,1)S(1)} %fusion.38, f32[2,512,512]{2,1,0:T(8,128)} %param.13), kind=kOutput, calls=%fused_computation.14 | convolution fusion | flops 6445596672 | bytes 11536384 | tf_op jit(solution)/shard_map/dot_general | solution.py:96
  272.0 2.5 maximum_select_fusion
  274.5 0.0 all-reduce.6.cloned.1.call-update
  274.5 0.3 all-reduce.8.cloned.1.call-start
  274.8 103.0 %all-reduce.6.cloned.1.call-done = bf16[2048,1024]{1,0:T(8,128)(2,1)} async-done(((bf16[2048,1024]{1,0:T(8,128)(2,1)}), bf16[2048,1024]{1,0:T(8,128)(2,1)}) %all-reduce.6.cloned.1.call-update) | async-done | bytes 4194320 | tf_op jit(solution)/shard_map/psum | solution.py:32
  377.7 3.5 fusion.14
  381.2 0.0 all-reduce.8.cloned.1.call-update
  381.3 65.9 %all-reduce.8.cloned.1.call-done = bf16[1024,1024]{1,0:T(8,128)(2,1)} async-done(((bf16[1024,1024]{1,0:T(8,128)(2,1)}), bf16[1024,1024]{1,0:T(8,128)(2,1)}) %all-reduce.8.cloned.1.call-update) | async-done | bytes 2097168 | tf_op jit(solution)/shard_map/psum | solution.py:32
  447.2 0.0 copy-start.1
  447.2 35.8 %select_select_fusion = f32[2048,1024]{1,0:T(8,128)} fusion(f32[2048,1024]{1,0:T(8,128)} %copy-done.2, bf16[1024,1024]{1,0:T(8,128)(2,1)} %all-reduce.8.cloned.1.call-done, pred[2048]{0:T(1024)(128)(4,1)S(1)} %get-tuple-element.11, pred[1024]{0:T(1024)(128)(4,1)S(1)} %get-tuple-element.14, pred[1024]{0:T(1024)(128)(4,1)S(1)} %get-tuple-element.13, ...), kind=kOutput, calls=%fused_computation.2 | convolution fusion | flops 25786580992 | bytes 23074816 | tf_op jit(solution)/shard_map/dot_general | solution.py:117
  482.9 0.0 copy-done.1
  (6 shorter events, 0.1 us)
Async XLA Ops:
  6.5 1.2 copy-start
  7.8 91.3 %copy-start.5 = (s32[1,64]{1,0:T(1,128)S(1)}, s32[1,64]{1,0:T(1,128)}, u32[]{:S(2)}) copy-start(s32[1,64]{1,0:T(1,128)} %param.11) | copy-start | bytes 772
  101.1 21.2 %all-to-all-start = ((bf16[8,64,1024]{2,1,0:T(8,128)(2,1)}), bf16[8,64,1024]{2,1,0:T(8,128)(2,1)S(1)}, u32[]{:S(2)}, u32[]{:S(2)}) async-start(bf16[8,64,1024]{2,1,0:T(8,128)(2,1)} %broadcast_in_dim.82), calls=%async_computation | async-start | bytes 2097152 | tf_op jit(solution)/shard_map/all_to_all | solution.py:23
  106.3 103.9 %all-reduce.10.cloned.1.call-start = ((), (), s32[]{:S(2)}) async-start(), calls=%async_computation.4 | async-start | bytes 4194304 | tf_op jit(solution)/shard_map/psum | solution.py:32
  123.8 134.3 %all-gather.3.cloned.1.call-start = ((), (), s32[]{:S(2)}) async-start(), calls=%async_computation.3 | async-start | bytes 4718592 | tf_op jit(solution)/shard_map/all_gather | solution.py:44
  210.3 6.8 %copy-start.4 = (f32[2,512,512]{2,1,0:T(8,128)S(1)}, f32[2,512,512]{2,1,0:T(8,128)}, u32[]{:S(2)}) copy-start(f32[2,512,512]{2,1,0:T(8,128)} %param.13) | copy-start | bytes 6291460
  217.0 8.3 %copy-start.2 = (f32[2048,1024]{1,0:T(8,128)}, f32[2048,1024]{1,0:T(8,128)S(1)}, u32[]{:S(2)}) copy-start(f32[2048,1024]{1,0:T(8,128)S(1)} %multiply_add_fusion) | copy-start | bytes 25165828
  226.2 151.5 %all-reduce.6.cloned.1.call-start = ((), (), s32[]{:S(2)}) async-start(), calls=%async_computation.1 | async-start | bytes 8388608 | tf_op jit(solution)/shard_map/psum | solution.py:32
  258.2 5.7 %copy-start.3 = (f32[2048,1024]{1,0:T(8,128)S(1)}, f32[2048,1024]{1,0:T(8,128)}, u32[]{:S(2)}) copy-start(f32[2048,1024]{1,0:T(8,128)} %copy-done.2) | copy-start | bytes 25165828
  274.5 172.7 %all-reduce.8.cloned.1.call-start = ((), (), s32[]{:S(2)}) async-start(), calls=%async_computation.2 | async-start | bytes 4194304 | tf_op jit(solution)/shard_map/psum | solution.py:32
  447.2 35.8 %copy-start.1 = (bf16[1024,512]{1,0:T(8,128)(2,1)S(1)}, bf16[1024,512]{1,0:T(8,128)(2,1)}, u32[]{:S(2)}) copy-start(bf16[1024,512]{1,0:T(8,128)(2,1)} %param.8) | copy-start | bytes 3145732
Sparse Core Ops, SparseCore 0:
  124.0 86.2 all-reduce.9
  226.4 31.7 all-gather.2
  274.6 103.0 all-reduce.5
  381.4 65.7 all-reduce.7
where the time goes:
time: 490 us; the launch traced here: 489 us
  waiting for transfers between devices  303 us (62%)
  blocking collectives  87.9 us (18%)
  matrix products  68 us (14%)
  between operations  13.3 us (3%)
  other arithmetic  7.93 us (2%)
  starting transfers between devices  5.8 us (1%)
    psum x3, waiting for transfers between devices, spread_2(): return lax.psum(jnp.where(mine, array, jnp.zeros_like(array)), axis)  255 us
    psum x1, blocking collectives, together(): running = lax.psum(jnp.concatenate([a.ravel() for a in arrays]), axis)  87.9 us
    dot_general x1, matrix products, per_device(): jnp.dot(lower_part, upper_part.T, precision=lax.Precision.HIGHEST)  35.8 us
    all_gather x1, waiting for transfers between devices, from_root(): lax.all_gather(array, axis)  31.7 us
    dot_general x2, matrix products, apply_inverse(): result = jnp.dot(columns, inverse.T, precision=lax.Precision.HIGHEST)  16.4 us
    all_to_all x1, waiting for transfers between devices, from_everyone(): return lax.all_to_all(copies, axis, split_axis=0, concat_axis=0, tiled=True)  15.9 us
  transfers between devices with their start and end apart: 5, of which 5 were waited for; matrix products, arithmetic and copies ran while one was open for 0% of the time, Pallas kernels for 0%

commit v1 on v0

--- a/solution.py
+++ b/solution.py
@@ -2,6 +2,12 @@
 import jax.numpy as jnp
 from jax import lax
 from jax.sharding import PartitionSpec as P
+
+
+def add_all(x, name):
+    parts = lax.all_gather(x, name, axis=0, tiled=False)
+    total = parts.sum(axis=0)
+    return total
 
 
 def together(arrays, axis):
@@ -29,7 +35,7 @@
 
 def spread_2(array, axis, root):
     mine = lax.axis_index(axis) == root
-    return lax.psum(jnp.where(mine, array, jnp.zeros_like(array)), axis)
+    return add_all(jnp.where(mine, array, jnp.zeros_like(array)), axis)
 
 
 def as_sent(array):

time: 490 us -> 957 us (1.95)
  waiting for transfers between devices: 303 us -> 711 us
  other arithmetic: 7.93 us -> 59.9 us
    all_gather x0 -> x4, waiting for transfers between devices: none -> 662 us  [add_all(): parts = lax.all_gather(x, name, axis=0, tiled=False)]
    psum x3 -> x0, waiting for transfers between devices: 255 us -> none  [spread_2(): return lax.psum(jnp.where(mine, array, jnp.zeros_like(array)), axis)]
    reduce_sum x0 -> x4, other arithmetic: none -> 51.9 us  [add_all(): total = parts.sum(axis=0)]
  transfers between devices with their start and end apart: 5 -> 6, of which waited for: 5 -> 6; matrix products, arithmetic and copies ran while one was open for 0% -> 1% of each run, Pallas kernels for 0% -> 0%
where the time goes in v1:
time: 957 us; the launch traced here: 955 us
  waiting for transfers between devices  711 us (74%)
  blocking collectives  87.9 us (9%)
  matrix products  67.5 us (7%)
  other arithmetic  59.9 us (6%)
  between operations  13.4 us (1%)
  local copies, waits for them, and re-layouts  10 us (1%)
    all_gather x4, waiting for transfers between devices, add_all(): parts = lax.all_gather(x, name, axis=0, tiled=False)  662 us
    psum x1, blocking collectives, together(): running = lax.psum(jnp.concatenate([a.ravel() for a in arrays]), axis)  87.9 us
    reduce_sum x4, other arithmetic, add_all(): total = parts.sum(axis=0)  51.9 us
    dot_general x1, matrix products, per_device(): jnp.dot(lower_part, upper_part.T, precision=lax.Precision.HIGHEST)  35.2 us
    all_gather x1, waiting for transfers between devices, from_root(): lax.all_gather(array, axis)  31.9 us
  transfers between devices with their start and end apart: 6, of which 6 were waited for; matrix products, arithmetic and copies ran while one was open for 1% of the time, Pallas kernels for 0%

profile of v1, /device:TPU:0, one launch (start us, length us, event | category | flops | bytes accessed | tf_op | source)
XLA Modules:
  0.0 955.4 jit_solution(8922338752593272164)
XLA Ops:
  6.5 0.0 copy-start
  6.5 1.2 copy-done
  7.8 0.0 copy-start.5
  7.8 1.3 convolution_bitcast_fusion
  9.1 1.7 convolution_bitcast_fusion.1
  10.8 0.1 pad_maximum_fusion
  10.8 87.9 %all-reduce.1 = bf16[262144]{0:T(1024)(128)(2,1)S(1)} all-reduce(f32[262144]{0:T(1024)S(1)} %pad_maximum_fusion), channel_id=1, replica_groups=mesh['row'=8,'col'=16] {'col'}, use_global_device_ids=true, to_apply=%region_1.0 | all-reduce | flops 262144 | bytes 1572864 | tf_op jit(solution)/shard_map/psum | solution.py:17
  98.8 0.1 constant_dynamic-slice_fusion
  98.9 0.1 copy.23
  99.0 0.0 copy-done.5
  99.1 0.1 copy.17
  99.1 0.1 reduce-window.4
  99.2 0.1 reduce.4
  99.4 0.1 fusion.37
  99.5 0.4 convolution_convert_fusion
  99.9 0.1 convert_element_type.51
  100.0 1.1 broadcast_in_dim.82
  101.1 5.2 all-to-all-start
  106.3 0.0 all-gather.8.cloned.1.call-start
  106.4 15.9 %all-to-all-done = bf16[8,64,1024]{2,1,0:T(8,128)(2,1)S(1)} async-done(((bf16[8,64,1024]{2,1,0:T(8,128)(2,1)}), bf16[8,64,1024]{2,1,0:T(8,128)(2,1)S(1)}, u32[]{:S(2)}, u32[]{:S(2)}) %all-to-all-start) | async-done | bytes 1048608 | tf_op jit(solution)/shard_map/all_to_all | solution.py:29
  122.3 1.5 broadcast_select_fusion.1
  123.7 0.0 all-gather.8.cloned.1.call-update
  123.8 0.0 all-gather.10.cloned.1.call-start
  123.8 0.7 all-gather.10.cloned.1.call-update
  124.5 0.0 all-gather.14.cloned.1.call-start
  124.6 105.7 %all-gather.8.cloned.1.call-done = bf16[16,512,1024]{2,1,0:T(8,128)(2,1)} async-done(((bf16[1,512,1024]{2,1,0:T(8,128)(2,1)}), bf16[16,512,1024]{2,1,0:T(8,128)(2,1)}) %all-gather.8.cloned.1.call-update) | async-done | bytes 16777232 | tf_op jit(solution)/shard_map/all_gather | solution.py:8
  230.3 9.3 reduce_sum.48
  239.6 103.6 %all-gather.10.cloned.1.call-done = bf16[16,512,1024]{2,1,0:T(8,128)(2,1)} async-done(((bf16[1,512,1024]{2,1,0:T(8,128)(2,1)}), bf16[16,512,1024]{2,1,0:T(8,128)(2,1)}) %all-gather.10.cloned.1.call-update) | async-done | bytes 16777232 | tf_op jit(solution)/shard_map/all_gather | solution.py:8
  343.2 9.3 reduce_sum.49
  352.6 0.0 copy-start.3
  352.6 6.1 multiply_add_fusion
  358.7 0.0 copy-done.3
  358.7 0.0 copy-start.2
  358.7 8.5 select_convert_fusion.1
  367.2 0.0 copy-done.2
  367.2 0.9 slice.55
  368.1 0.0 all-gather.14.cloned.1.call-update
  368.1 0.2 all-gather.12.cloned.1.call-start
  368.4 31.9 %all-gather.14.cloned.1.call-done = bf16[4096,512]{0,1:T(8,128)(2,1)} async-done(((bf16[512,512]{0,1:T(8,128)(2,1)}), bf16[4096,512]{0,1:T(8,128)(2,1)}) %all-gather.14.cloned.1.call-update) | async-done | bytes 4194320 | tf_op jit(solution)/shard_map/all_gather | solution.py:50
  400.2 0.0 copy-start.4
  400.2 5.6 fusion.9
  405.8 0.0 copy-done.4
  405.8 8.7 fusion.14
  414.5 2.6 maximum_select_fusion
  417.1 6.4 copy.19
  423.5 0.0 all-gather.12.cloned.1.call-update
  423.5 0.3 all-gather.16.cloned.1.call-start
  423.8 368.1 %all-gather.12.cloned.1.call-done = bf16[16,2048,1024]{2,1,0:T(8,128)(2,1)} async-done(((bf16[1,2048,1024]{2,1,0:T(8,128)(2,1)}), bf16[16,2048,1024]{2,1,0:T(8,128)(2,1)}) %all-gather.12.cloned.1.call-update) | async-done | bytes 67108880 | tf_op jit(solution)/shard_map/all_gather | solution.py:8
  791.9 23.8 %reduce_sum.50 = bf16[2048,1024]{1,0:T(8,128)(2,1)} reduce(bf16[16,2048,1024]{2,1,0:T(8,128)(2,1)} %all-gather.12.cloned.1.call-done, bf16[]{:T(256)} %constant.70.clone.1), dimensions={0}, to_apply=%region_4.5 | reduce | flops 31457280 | bytes 71303168 | tf_op jit(solution)/shard_map/reduce_sum | solution.py:9
  815.7 3.5 fusion.15
  819.1 0.0 all-gather.16.cloned.1.call-update
  819.2 84.9 %all-gather.16.cloned.1.call-done = bf16[8192,1024]{1,0:T(8,128)(2,1)} async-done(((bf16[1024,1024]{1,0:T(8,128)(2,1)}), bf16[8192,1024]{1,0:T(8,128)(2,1)}) %all-gather.16.cloned.1.call-update) | async-done | bytes 16777232 | tf_op jit(solution)/shard_map/all_gather | solution.py:8
  904.1 9.5 reduce_sum.51
  913.6 0.0 copy-start.1
  913.6 35.2 %select_select_fusion = f32[2048,1024]{1,0:T(8,128)} fusion(f32[2048,1024]{1,0:T(8,128)} %copy-done.2, bf16[1024,1024]{1,0:T(8,128)(2,1)S(1)} %reduce_sum.51, pred[2048]{0:T(1024)(128)(4,1)S(1)} %get-tuple-element.9, pred[1024]{0:T(1024)(128)(4,1)S(1)} %get-tuple-element.12, pred[1024]{0:T(1024)(128)(4,1)S(1)} %get-tuple-element.11, ...), kind=kOutput, calls=%fused_computation.2 | convolution fusion | flops 25786580992 | bytes 23074816 | tf_op jit(solution)/shard_map/dot_general | solution.py:123
  948.8 0.0 copy-done.1
  (6 shorter events, 0.1 us)
Async XLA Ops:
  6.5 1.2 copy-start
  7.8 91.3 %copy-start.5 = (s32[1,64]{1,0:T(1,128)S(1)}, s32[1,64]{1,0:T(1,128)}, u32[]{:S(2)}) copy-start(s32[1,64]{1,0:T(1,128)} %param.11) | copy-start | bytes 772
  101.1 21.2 %all-to-all-start = ((bf16[8,64,1024]{2,1,0:T(8,128)(2,1)}), bf16[8,64,1024]{2,1,0:T(8,128)(2,1)S(1)}, u32[]{:S(2)}, u32[]{:S(2)}) async-start(bf16[8,64,1024]{2,1,0:T(8,128)(2,1)} %broadcast_in_dim.82), calls=%async_computation | async-start | bytes 2097152 | tf_op jit(solution)/shard_map/all_to_all | solution.py:29
  106.3 124.0 %all-gather.8.cloned.1.call-start = ((), (), s32[]{:S(2)}) async-start(), calls=%async_computation.1 | async-start | bytes 17825792 | tf_op jit(solution)/shard_map/all_gather | solution.py:8
  123.8 219.5 %all-gather.10.cloned.1.call-start = ((), (), s32[]{:S(2)}) async-start(), calls=%async_computation.2 | async-start | bytes 17825792 | tf_op jit(solution)/shard_map/all_gather | solution.py:8
  124.5 275.7 %all-gather.14.cloned.1.call-start = ((), (), s32[]{:S(2)}) async-start(), calls=%async_computation.4 | async-start | bytes 4718592 | tf_op jit(solution)/shard_map/all_gather | solution.py:50
  352.6 6.1 copy-start.3
  358.7 8.5 copy-start.2
  368.1 423.8 %all-gather.12.cloned.1.call-start = ((), (), s32[]{:S(2)}) async-start(), calls=%async_computation.3 | async-start | bytes 71303168 | tf_op jit(solution)/shard_map/all_gather | solution.py:8
  400.2 5.6 copy-start.4
  423.5 480.6 %all-gather.16.cloned.1.call-start = ((), (), s32[]{:S(2)}) async-start(), calls=%async_computation.5 | async-start | bytes 18874368 | tf_op jit(solution)/shard_map/all_gather | solution.py:8
  913.6 35.3 %copy-start.1 = (bf16[1024,512]{1,0:T(8,128)(2,1)S(1)}, bf16[1024,512]{1,0:T(8,128)(2,1)}, u32[]{:S(2)}) copy-start(bf16[1024,512]{1,0:T(8,128)(2,1)} %param.8) | copy-start | bytes 3145732
Sparse Core Ops, SparseCore 0:
  123.9 106.3 all-gather.7
  232.4 110.7 all-gather.9
  368.2 31.9 all-gather.13
  423.6 368.1 all-gather.11
  819.3 84.8 all-gather.15
